TPU v7x, 256 devices: a whole 4x4x8 slice. The times are simulated.
256 devices in a mesh: rows: 64 (over z, y, core), mem: 4 (over x).
Axes of the slice: x: 4, y: 4, z: 8, core: 2. Of those that a mesh axis runs over, the one named last changes fastest.
Arguments:
- control: bfloat16 [16, 32, 2, 512, 512], P('mem', None, None, 'rows'), may hold values from -6 to 6
- vert_root: float32 [32, 32], replicated, may hold values from -1 to 1
- loc_spec: float32 [512], replicated, may hold values from 0.1 to 1
- legendre: bfloat16 [512, 512, 768], P('rows'), as said below
- wave_table: int32 [512], replicated, may hold values from 0 to 511, as said below
- lat_order: int32 [768], replicated, may hold values from 0 to 767, each once
- perturb: bfloat16 [768, 16, 32, 1536], P('rows', None, 'mem'), may hold values from -3 to 3
Outputs:
- increment: bfloat16 [768, 32, 1536], P('rows', 'mem')
Inputs may be any that keep to these rules, and one draw needn't show every extreme that they name: `wave_table`: every zonal wavenumber 0 to 511 sits in exactly one slot; the slots held by one index of rows are pairs m and 511 - m. legendre[s, n, t] is zero where n < wave_table[s]. `lat_order`: a permutation.
All inputs are finite; a program needn't handle non-finite values.
Results may differ from a plain program's by a relative error of at most 0.0085.
Values may be sent and summed in bfloat16 or wider, within the bound.
A program may use at most 128 MiB of HBM per device.

v0:
```python
import math

import jax
import jax.numpy as jnp
from jax import lax
from jax.sharding import PartitionSpec as P


def make_basis(wave_table, lon_count):
    longitude = lax.iota(jnp.int32, lon_count)
    phases = wave_table[:, None] * longitude[None, :] % lon_count
    angles = phases.astype(jnp.float32) * (2.0 * math.pi / lon_count)
    weights = jnp.where(wave_table == 0, 1.0, 2.0).astype(jnp.float32)[:, None]
    return jnp.stack([weights * jnp.cos(angles), -weights * jnp.sin(angles)]).astype(jnp.bfloat16)


def synthesize(level_block, legendre, lat_order, zonal_basis):
    fourier = jnp.einsum(
        "snt,klrsn->strkl", legendre, level_block, preferred_element_type=jnp.float32
    )
    fourier = jnp.take(fourier, lat_order, axis=1)
    four_shape = fourier.shape
    fourier = fourier.reshape(four_shape[0], four_shape[1], -1).astype(jnp.bfloat16)
    fourier = lax.all_to_all(fourier, "rows", split_axis=1, concat_axis=0, tiled=True)
    fourier = fourier.reshape(
        fourier.shape[0], fourier.shape[1], four_shape[2], four_shape[3], four_shape[4]
    )
    fields = jnp.einsum("sjrkl,rsx->jklx", fourier, zonal_basis, preferred_element_type=jnp.float32)
    return fields.astype(jnp.bfloat16)


def member_sum(fields, member_ptb):
    return jnp.sum(fields.astype(jnp.float32) * member_ptb.astype(jnp.float32), axis=1)


def shards(control, vert_root, loc_spec, legendre, wave_table, lat_order, perturb):
    mem_count = lax.axis_size("mem")
    members_dev, levels, _, slot_count, wave_count = control.shape
    level_share = levels // mem_count
    batch_count = 1
    level_batch = level_share // batch_count
    scaled = control.astype(jnp.float32) * loc_spec
    spectra = jnp.einsum(
        "lv,kvrsn->klrsn", vert_root, scaled, precision=lax.Precision.HIGHEST
    ).astype(jnp.bfloat16)
    zonal_basis = make_basis(wave_table, perturb.shape[3])
    grouped = spectra.reshape(
        members_dev, mem_count, batch_count, level_batch, 2, slot_count, wave_count
    )
    level_block = grouped[:, :, 0].reshape(
        members_dev, mem_count * level_batch, 2, slot_count, wave_count
    )
    fields = synthesize(level_block, legendre, lat_order, zonal_basis)
    fields = lax.all_to_all(fields, "mem", split_axis=2, concat_axis=1, tiled=True)
    pieces = member_sum(fields, perturb)
    return pieces.astype(jnp.bfloat16)


def solution(mesh):
    return jax.shard_map(
        shards,
        mesh=mesh,
        in_specs=(
            P("mem", None, None, "rows", None),
            P(),
            P(),
            P("rows", None, None),
            P(),
            P(),
            P("rows", None, "mem", None),
        ),
        out_specs=P("rows", "mem", None),
        check_vma=False,
    )
```

profile of v0, /device:TPU:1, one launch (start us, length us, event | category | flops | bytes accessed | tf_op | source)
XLA Modules:
  0.0 268.7 jit_solution(8176446546091429592)
XLA Ops:
  0.0 0.0 copy-start
  0.0 0.7 compare_select_fusion
  0.7 0.7 compare_and_fusion
  1.4 0.0 slice-start
  1.4 2.4 convert_multiply_fusion
  3.8 0.0 copy-done
  3.8 0.0 slice-start.1
  3.8 7.2 %fusion.7 = bf16[4,2,8,512,32]{3,4,1,0,2:T(8,128)(2,1)S(1)} fusion(f32[4,32,2,8,512]{4,3,2,1,0:T(8,128)S(1)} %convert_multiply_fusion, f32[32,32]{1,0:T(8,128)S(1)} %copy-done), kind=kOutput, calls=%fused_computation.11 | convolution fusion | flops 402653184 | bytes 6295552 | tf_op jit(solution)/shard_map/lv,kvrsn->klrsn/dot_general | solution.py:43
  11.0 0.0 slice-done
  11.0 0.0 slice-done.1
  11.0 1.8 fusion.16
  12.9 17.4 %copy.16 = bf16[8,768,2,4,32]{4,0,3,2,1:T(8,128)(2,1)} copy(bf16[8,768,2,4,32]{1,4,2,3,0:T(8,128)(2,1)S(1)} %fusion.16) | data formatting | bytes 6291456 | tf_op jit(solution)/shard_map/snt,klrsn->strkl/transpose | solution.py:18
  30.3 24.4 %gather_fusion = bf16[768,8,2,4,32]{4,1,3,2,0:T(8,128)(2,1)} fusion(bf16[8,768,2,4,32]{4,0,3,2,1:T(8,128)(2,1)} %copy.16, s32[1024]{0:T(1024)S(1)} %pad_clamp_fusion), kind=kCustom, calls=%fused_computation | custom fusion | bytes 6294528 | tf_op jit(solution)/shard_map/jit(_take)/gather | solution.py:21
  54.7 14.6 %copy.17 = bf16[8,768,2,4,32]{1,4,3,2,0:T(8,128)(2,1)} copy(bf16[8,768,2,4,32]{4,0,3,2,1:T(8,128)(2,1)} %bitcast.42) | data formatting | bytes 6291456 | tf_op jit(solution)/shard_map/jit(_take)/gather | solution.py:21
  69.2 2.4 fusion.4
  71.7 3.5 %copy.18 = bf16[8,768,256]{2,0,1:T(8,128)(2,1)} copy(bf16[8,768,256]{1,2,0:T(8,128)(2,1)S(1)} %fusion.4) | data formatting | bytes 6291456 | tf_op jit(solution)/shard_map/convert_element_type | solution.py:23
  75.1 0.0 copy-start.4
  75.1 13.3 %all-to-all-start = ((bf16[8,768,256]{2,0,1:T(8,128)(2,1)}), bf16[8,768,256]{2,0,1:T(8,128)(2,1)S(1)}, u32[]{:S(2)}, u32[]{:S(2)}) async-start(bf16[8,768,256]{2,0,1:T(8,128)(2,1)} %copy.18), calls=%async_computation | async-start | bytes 6291456 | tf_op jit(solution)/shard_map/all_to_all | solution.py:24
  88.4 0.0 copy-done.4
  88.4 15.3 %multiply_convert_fusion.1 = (bf16[1,512,1536]{2,1,0:T(8,128)(2,1)}, bf16[1,512,1536]{2,1,0:T(8,128)(2,1)}) fusion(s32[512]{0:T(512)S(1)} %copy-done.4, f32[512]{0:T(512)S(1)} %get-tuple-element.7, f32[512]{0:T(512)S(1)} %get-tuple-element.8), kind=kLoop, calls=%fused_computation.20 | loop fusion | flops 10223616 | bytes 3151872 | tf_op jit(solution)/shard_map/convert.3
  103.7 57.1 %all-to-all-done = bf16[8,768,256]{2,0,1:T(8,128)(2,1)S(1)} async-done(((bf16[8,768,256]{2,0,1:T(8,128)(2,1)}), bf16[8,768,256]{2,0,1:T(8,128)(2,1)S(1)}, u32[]{:S(2)}, u32[]{:S(2)}) %all-to-all-start) | async-done | bytes 3145760 | tf_op jit(solution)/shard_map/all_to_all | solution.py:24
  160.8 1.9 copy.19
  162.7 0.0 copy-start.2
  162.7 0.0 copy-start.3
  162.7 17.2 %reshape.137 = bf16[512,12,2,4,32]{4,3,2,0,1:T(4,128)(2,1)} reshape(bf16[64,8,12,256]{3,1,0,2:T(8,128)(2,1)} %copy.19) | data formatting | bytes 6291456 | tf_op jit(solution)/shard_map/reshape | solution.py:25
  179.9 0.0 copy-done.2
  179.9 0.0 copy-done.3
  179.9 8.9 %bitcast_convert_fusion = bf16[12,4,32,1536]{3,2,1,0:T(8,128)(2,1)S(1)} fusion(bf16[512,12,2,4,32]{4,3,2,0,1:T(4,128)(2,1)} %reshape.137, bf16[1,512,1536]{2,1,0:T(8,128)(2,1)S(1)} %copy-done.3, bf16[1,512,1536]{2,1,0:T(8,128)(2,1)S(1)} %copy-done.2), kind=kOutput, calls=%fused_computation.4 | convolution fusion | flops 4835770368 | bytes 11010048 | tf_op jit(solution)/shard_map/sjrkl,rsx->jklx/dot_general | solution.py:28
  188.9 3.6 %copy.21 = bf16[12,4,32,1536]{3,1,0,2:T(4,128)(2,1)S(1)} copy(bf16[12,4,32,1536]{3,2,1,0:T(8,128)(2,1)S(1)} %bitcast_convert_fusion) | data formatting | bytes 9437184 | tf_op jit(solution)/shard_map/convert_element_type | solution.py:29
  192.5 56.0 %all_to_all.24 = bf16[12,4,32,1536]{3,1,0,2:T(4,128)(2,1)} all-to-all(bf16[12,4,32,1536]{3,1,0,2:T(4,128)(2,1)S(1)} %copy.21), channel_id=1, replica_groups=mesh['rows'=64,'mem'=4] {'mem'}, dimensions={2} | all-to-all | bytes 9437184 | tf_op jit(solution)/shard_map/all_to_all | solution.py:54
  248.5 3.8 %convert_bitcast_fusion = f32[12,4,4,8,1536]{4,2,0,3,1:T(4,128)S(1)} fusion(bf16[12,4,4,8,1536]{4,1,0,3,2:T(4,128)(2,1)} %bitcast.44), kind=kLoop, calls=%fused_computation.3 | loop fusion | flops 2359296 | bytes 14155776 | tf_op jit(solution)/shard_map/convert_element_type | solution.py:33
  252.3 9.1 %copy.22 = f32[12,4,4,8,1536]{4,3,2,1,0:T(8,128)} copy(f32[12,4,4,8,1536]{4,2,0,3,1:T(4,128)S(1)} %convert_bitcast_fusion) | data formatting | bytes 18874368 | tf_op jit(solution)/shard_map/convert_element_type | solution.py:33
  261.4 0.0 copy-start.1
  261.4 7.3 %multiply_reduce_fusion = bf16[12,8,1536]{2,1,0:T(8,128)(2,1)} fusion(f32[12,16,8,1536]{3,2,1,0:T(8,128)} %bitcast.43, bf16[12,16,8,1536]{3,2,1,0:T(8,128)(2,1)} %param.13), kind=kLoop, calls=%fused_computation.5 | loop fusion | flops 6930432 | bytes 14450688 | tf_op jit(solution)/shard_map/reduce_sum | solution.py:33
  268.7 0.0 copy-done.1
  (3 shorter events, 0.0 us)
Async XLA Ops:
  0.0 3.8 %copy-start = (f32[32,32]{1,0:T(8,128)S(1)}, f32[32,32]{1,0:T(8,128)}, u32[]{:S(2)}) copy-start(f32[32,32]{1,0:T(8,128)} %param.8) | copy-start | bytes 12292
  1.4 9.6 %slice-start = ((s8[6291456]{0:T(1024)(128)(4,1)}), s8[4194304]{0:T(1024)(128)(4,1)S(1)}, s32[]{:S(2)}) async-start(s8[6291456]{0:T(1024)(128)(4,1)} %bitcast.46), calls=%async_computation.2 | async-start | bytes 8388608
  3.8 7.2 %slice-start.1 = ((s8[6291456]{0:T(1024)(128)(4,1)}), s8[2097152]{0:T(1024)(128)(4,1)S(1)}, s32[]{:S(2)}) async-start(s8[6291456]{0:T(1024)(128)(4,1)} %bitcast.46), calls=%async_computation.3 | async-start | bytes 4194304
  75.1 13.3 %copy-start.4 = (s32[512]{0:T(512)S(1)}, s32[512]{0:T(512)}, u32[]{:S(2)}) copy-start(s32[512]{0:T(512)} %param.11) | copy-start | bytes 6148
  75.1 85.7 %all-to-all-start = ((bf16[8,768,256]{2,0,1:T(8,128)(2,1)}), bf16[8,768,256]{2,0,1:T(8,128)(2,1)S(1)}, u32[]{:S(2)}, u32[]{:S(2)}) async-start(bf16[8,768,256]{2,0,1:T(8,128)(2,1)} %copy.18), calls=%async_computation | async-start | bytes 6291456 | tf_op jit(solution)/shard_map/all_to_all | solution.py:24
  162.7 17.2 %copy-start.2 = (bf16[1,512,1536]{2,1,0:T(8,128)(2,1)S(1)}, bf16[1,512,1536]{2,1,0:T(8,128)(2,1)}, u32[]{:S(2)}) copy-start(bf16[1,512,1536]{2,1,0:T(8,128)(2,1)} %get-tuple-element.5) | copy-start | bytes 4718596
  162.7 17.2 %copy-start.3 = (bf16[1,512,1536]{2,1,0:T(8,128)(2,1)S(1)}, bf16[1,512,1536]{2,1,0:T(8,128)(2,1)}, u32[]{:S(2)}) copy-start(bf16[1,512,1536]{2,1,0:T(8,128)(2,1)} %get-tuple-element.6) | copy-start | bytes 4718596
  261.4 7.3 %copy-start.1 = (f32[32,32]{1,0:T(8,128)S(1)}, f32[32,32]{1,0:T(8,128)}, u32[]{:S(2)}) copy-start(f32[32,32]{1,0:T(8,128)} %param.8) | copy-start | bytes 12292
where the time goes:
time: 271 us; the launch traced here: 269 us
  local copies, waits for them, and re-layouts  91.7 us (34%)
  waiting for transfers between devices  57.1 us (21%)
  blocking collectives  56 us (21%)
  other arithmetic  32.6 us (12%)
  matrix products  17.9 us (7%)
  starting transfers between devices  13.3 us (5%)
    all_to_all x1, waiting for transfers between devices, synthesize(): lax.all_to_all(fourier, 'rows', split_axis=1, concat_axis=0, tiled=True)  57.1 us
    all_to_all x1, blocking collectives, shards(): lax.all_to_all(fields, 'mem', split_axis=2, concat_axis=1, tiled=True)  56 us
    gather x2, local copies, waits for them, and re-layouts, synthesize(): fourier = jnp.take(fourier, lat_order, axis=1)  39 us
    transpose x1, local copies, waits for them, and re-layouts, synthesize(): jnp.einsum('snt,klrsn->strkl', legendre, level_block, preferred_element_t...  17.4 us
    reshape x1, local copies, waits for them, and re-layouts, synthesize(): fourier.reshape(fourier.shape[0], fourier.shape[1], four_shape[2], four_s...  17.2 us
    another operation x1, other arithmetic  15.3 us
    all_to_all x1, starting transfers between devices, synthesize(): lax.all_to_all(fourier, 'rows', split_axis=1, concat_axis=0, tiled=True)  13.3 us
    convert_element_type x1, local copies, waits for them, and re-layouts, member_sum(): fields.astype(jnp.float32) * member_ptb.astype(jnp.float32)  9.1 us
  transfers between devices with their start and end apart: 1, of which 1 were waited for; matrix products, arithmetic and copies ran while one was open for 6% of the time, Pallas kernels for 0%

commit v1 on v0

v1 whole, which is shorter than its diff:
```python
import functools
import math

import jax
import jax.numpy as jnp
from jax import lax
from jax.experimental import pallas as pl
from jax.experimental.pallas import tpu as pltpu
from jax.sharding import PartitionSpec as P

MESH = pl.DeviceIdType.MESH
F32, BF16 = jnp.float32, jnp.bfloat16
NT_DIMS = (((1,), (1,)), ((), ()))


def dot(a, b):
    return jnp.dot(a, b, preferred_element_type=F32)


def split3(a):
    hi = a.astype(BF16)
    rest = a - hi.astype(F32)
    mid = rest.astype(BF16)
    low = (rest - mid.astype(F32)).astype(BF16)
    return hi, mid, low


def spread_rows(row):
    return jnp.transpose(jnp.broadcast_to(row, (128, 128)))


def peer(row, mem, o):
    z, y, c = lax.div(row, 8), lax.rem(lax.div(row, 2), 4), lax.rem(row, 2)
    z = lax.rem(z + lax.div(o, 32), 8)
    y = lax.rem(y + lax.rem(lax.div(o, 8), 4), 4)
    c = lax.rem(c + lax.rem(lax.div(o, 4), 2), 2)
    return (z * 4 + y) * 2 + c, lax.rem(mem + lax.rem(o, 4), 4)


def kernel(
    control, root, loc, legendre, waves, order, perturb, out,
    ctrl, leg, pert, sp32, spec, four, latf, onehot, msg, snd, rcv, wavef, basis, lhs,
    in_sem, leg_sem, send_sem, recv_sem,
):
    row, mem = lax.axis_index("rows"), lax.axis_index("mem")
    barrier = pltpu.get_barrier_semaphore()

    for k in range(4):
        pltpu.make_async_copy(control.at[k], ctrl.at[k], in_sem.at[k]).start()

    def load_leg(s, _):
        pltpu.make_async_copy(legendre.at[s], leg.at[s], leg_sem.at[s]).start()
        return 0

    lax.fori_loop(0, 8, load_leg, 0)
    pltpu.make_async_copy(perturb, pert, in_sem.at[4]).start()

    def greet(o, _):
        r, m = peer(row, mem, o)
        pl.semaphore_signal(barrier, inc=1, device_id=(r, m), device_id_type=MESH)
        return 0

    lax.fori_loop(1, 256, greet, 0)

    pick = (
        lax.broadcasted_iota(jnp.int32, (256, 32), 0) % 32
        == lax.broadcasted_iota(jnp.int32, (256, 32), 1)
    ).astype(F32).astype(BF16)
    widen = (
        lax.broadcasted_iota(jnp.int32, (32, 256), 1) // 8
        == lax.broadcasted_iota(jnp.int32, (32, 256), 0)
    ).astype(F32).astype(BF16)
    same = (
        lax.broadcasted_iota(jnp.int32, (256, 256), 0) // 32
        == lax.broadcasted_iota(jnp.int32, (256, 256), 1) % 8
    )
    mix = [
        jnp.where(same, dot(dot(pick, part).astype(BF16), widen), 0.0).astype(BF16)
        for part in split3(root[...])
    ]

    for b in range(6):
        latf[b * 128:(b + 1) * 128, :] = spread_rows(order[b:b + 1, :].astype(F32))
    lane = lax.broadcasted_iota(jnp.int32, (64, 128), 1)
    lane_f = lane.astype(F32)
    for c in range(3):
        for q in range(4):
            rows = latf[pl.ds(c * 4 + q, 64, stride=12), :]
            for b in range(6):
                hit = rows == lane_f + float(b * 128)
                onehot[c, q * 64:(q + 1) * 64, b * 128:(b + 1) * 128] = jnp.where(
                    hit, 1.0, 0.0
                ).astype(BF16)

    for k in range(4):
        pltpu.make_async_copy(control.at[k], ctrl.at[k], in_sem.at[k]).wait()
    scale = loc[...]
    for r in range(2):
        for k in range(4):
            x = ctrl[k, :, r].reshape(256, 512)
            mixed = (dot(mix[0], x) + dot(mix[1], x) + dot(mix[2], x)) * scale
            sp32[:, :, k] = mixed.reshape(8, 4, 8, 512)

        def narrow(s, _):
            spec[s, r * 128:(r + 1) * 128, :] = sp32[s].reshape(128, 512).astype(BF16)
            return 0

        lax.fori_loop(0, 8, narrow, 0)

    def transform(s, _):
        pltpu.make_async_copy(legendre.at[s], leg.at[s], leg_sem.at[s]).wait()
        four[s] = dot(spec[s], leg[s]).astype(BF16)
        return 0

    lax.fori_loop(0, 8, transform, 0)

    group = lane // 32
    me = mem * 64 + row
    pl.semaphore_wait(barrier, 255)

    def build(c, _):
        def one(s, _):
            picked = lax.dot_general(onehot[c], four[s], NT_DIMS, preferred_element_type=F32)
            for r in range(2):
                rolled = []
                for q in range(4):
                    part = picked[q * 64:(q + 1) * 64, r * 128:(r + 1) * 128]
                    rolled.append(pltpu.roll(part, q * 32, 1) if q else part)
                for level in range(4):
                    tile = rolled[(0 - level) % 4]
                    for g in range(1, 4):
                        tile = jnp.where(group == g, rolled[(g - level) % 4], tile)
                    msg[pl.ds(level * 16 + r * 8 + s, 64, stride=64), :] = tile
            return 0

        lax.fori_loop(0, 8, one, 0)

        def pack(b, _):
            start = pl.multiple_of(b * 512, 512)
            snd[c, pl.ds(b * 32, 32)] = msg[pl.ds(start, 512), :].reshape(32, 16, 128).astype(BF16)
            return 0

        lax.fori_loop(0, 8, pack, 0)

        def send(o, _):
            r, m = peer(row, mem, o)
            pltpu.make_async_remote_copy(
                src_ref=snd.at[c, r * 4 + m],
                dst_ref=rcv.at[c, me],
                send_sem=send_sem.at[c],
                recv_sem=recv_sem.at[c],
                device_id=(r, m),
                device_id_type=MESH,
            ).start()
            return 0

        lax.fori_loop(1, 256, send, 0)
        rcv[c, me] = snd[c, row * 4 + mem]
        return 0

    lax.fori_loop(0, 3, build, 0)

    for b in range(4):
        wavef[b * 128:(b + 1) * 128, :] = spread_rows(waves[b:b + 1, :].astype(F32))

    def angles(wave, step):
        phase = wave * step
        phase = phase - 1536.0 * jnp.floor(phase * (1.0 / 1536.0))
        return phase * (2.0 * math.pi / 1536.0)

    def make_basis(b, _):
        wave = wavef[pl.ds(pl.multiple_of(b * 64, 64), 64), :]
        weight = jnp.where(wave == 0.0, 1.0, 2.0)
        near = angles(wave, lane_f)
        far = angles(wave, 128.0)
        cos, sin = weight * jnp.cos(near), weight * jnp.sin(near)
        turn_cos, turn_sin = jnp.cos(far), jnp.sin(far)
        for a in range(12):
            pair = jnp.stack([cos.reshape(8, 8, 128), -sin.reshape(8, 8, 128)], axis=1)
            basis[pl.ds(pl.multiple_of(b * 128, 128), 128), a * 128:(a + 1) * 128] = (
                pair.reshape(128, 128).astype(BF16)
            )
            cos, sin = cos * turn_cos - sin * turn_sin, sin * turn_cos + cos * turn_sin
        return 0

    lax.fori_loop(0, 8, make_basis, 0)
    pltpu.make_async_copy(perturb, pert, in_sem.at[4]).wait()

    def finish(c, _):
        pltpu.make_async_copy(
            rcv.at[c, pl.ds(0, 255)], rcv.at[c, pl.ds(0, 255)], recv_sem.at[c]
        ).wait()
        for kg in range(4):
            lhs[kg * 128:(kg + 1) * 128, :] = jnp.transpose(
                rcv[c, kg * 64:(kg + 1) * 64].reshape(1024, 128)
            )

        def columns(n, _):
            cols = pl.ds(pl.multiple_of(n * 256, 256), 256)
            field = dot(lhs[...], basis[:, cols]).astype(BF16).astype(F32)
            field = field.reshape(4, 4, 4, 8, 256)
            for g in range(4):
                j = c * 4 + lax.rem(g + 4 - mem, 4)
                weights = pert[j, :, :, cols].astype(F32).reshape(4, 4, 8, 256)
                out[j, :, cols] = jnp.sum(field[:, g] * weights, axis=(0, 1)).astype(BF16)
            return 0

        lax.fori_loop(0, 6, columns, 0)
        pltpu.make_async_copy(
            snd.at[c, pl.ds(0, 255)], snd.at[c, pl.ds(0, 255)], send_sem.at[c]
        ).wait()
        return 0

    lax.fori_loop(0, 3, finish, 0)


def shards(control, vert_root, loc_spec, legendre, wave_table, lat_order, perturb):
    vmem = pl.BlockSpec(memory_space=pltpu.VMEM)
    hbm = pl.BlockSpec(memory_space=pl.ANY)
    return pl.pallas_call(
        kernel,
        name="synthesis",
        out_shape=jax.ShapeDtypeStruct((12, 8, 1536), BF16),
        in_specs=[hbm, vmem, vmem, hbm, vmem, vmem, hbm],
        out_specs=vmem,
        scratch_shapes=[
            pltpu.VMEM((4, 32, 2, 8, 512), BF16),
            pltpu.VMEM((8, 512, 768), BF16),
            pltpu.VMEM((12, 16, 8, 1536), BF16),
            pltpu.VMEM((8, 4, 4, 8, 512), F32),
            pltpu.VMEM((8, 256, 512), BF16),
            pltpu.VMEM((8, 256, 768), BF16),
            pltpu.VMEM((768, 128), F32),
            pltpu.VMEM((3, 256, 768), BF16),
            pltpu.VMEM((4096, 128), F32),
            pltpu.VMEM((3, 256, 16, 128), BF16),
            pltpu.VMEM((3, 256, 16, 128), BF16),
            pltpu.VMEM((512, 128), F32),
            pltpu.VMEM((1024, 1536), BF16),
            pltpu.VMEM((512, 1024), BF16),
            pltpu.SemaphoreType.DMA((5,)),
            pltpu.SemaphoreType.DMA((8,)),
            pltpu.SemaphoreType.DMA((3,)),
            pltpu.SemaphoreType.DMA((3,)),
        ],
        compiler_params=pltpu.CompilerParams(
            collective_id=0, has_side_effects=True, vmem_limit_bytes=60 * 1024 * 1024
        ),
    )(
        control, vert_root, loc_spec.reshape(1, 512), legendre,
        wave_table.reshape(4, 128), lat_order.reshape(6, 128), perturb,
    )


def solution(mesh):
    return jax.shard_map(
        shards,
        mesh=mesh,
        in_specs=(
            P("mem", None, None, "rows", None),
            P(),
            P(),
            P("rows", None, None),
            P(),
            P(),
            P("rows", None, "mem", None),
        ),
        out_specs=P("rows", "mem", None),
        check_vma=False,
    )
```

time: 271 us -> 107 us (0.39)
  Pallas kernels: 0 us -> 105 us
  local copies, waits for them, and re-layouts: 91.7 us -> 1.69 us
  waiting for transfers between devices: 57.1 us -> 0 us
  blocking collectives: 56 us -> 0 us
  other arithmetic: 32.6 us -> 0 us
  matrix products: 17.9 us -> 0 us
  starting transfers between devices: 13.3 us -> 0 us
    pallas_call x0 -> x1, Pallas kernels: none -> 105 us  [shards(): pl.pallas_call(kernel, name='synthesis', out_shape=jax.ShapeDtypeStruct((...]
    all_to_all x1 -> x0, waiting for transfers between devices: 57.1 us -> none  [synthesize(): lax.all_to_all(fourier, 'rows', split_axis=1, concat_axis=0, tiled=True)]
    all_to_all x1 -> x0, blocking collectives: 56 us -> none  [shards(): lax.all_to_all(fields, 'mem', split_axis=2, concat_axis=1, tiled=True)]
    gather x2 -> x0, local copies, waits for them, and re-layouts: 39 us -> none  [synthesize(): fourier = jnp.take(fourier, lat_order, axis=1)]
    dot_general x3 -> x0, matrix products: 17.9 us -> none  [the longest x1 8.91 us: synthesize(): jnp.einsum('sjrkl,rsx->jklx', fourier, zonal_basis, preferred_element_typ...]
    transpose x1 -> x0, local copies, waits for them, and re-layouts: 17.4 us -> none  [synthesize(): jnp.einsum('snt,klrsn->strkl', legendre, level_block, preferred_element_t...]
    reshape x1 -> x0, local copies, waits for them, and re-layouts: 17.2 us -> none  [synthesize(): fourier.reshape(fourier.shape[0], fourier.shape[1], four_shape[2], four_s...]
    convert_element_type x3 -> x0, local copies, waits for them, and re-layouts: 16.2 us -> none  [the longest x1 9.1 us: member_sum(): fields.astype(jnp.float32) * member_ptb.astype(jnp.float32)]
  transfers between devices with their start and end apart: 1 -> 0, of which waited for: 1 -> 0; matrix products, arithmetic and copies ran while one was open for 6% -> 0% of each run, Pallas kernels for 0% -> 0%
where the time goes in v1:
time: 107 us
  Pallas kernels  105 us (98%)
  local copies, waits for them, and re-layouts  1.69 us (2%)
    pallas_call x1, Pallas kernels, shards(): pl.pallas_call(kernel, name='synthesis', out_shape=jax.ShapeDtypeStruct((...  105 us

profile of v1, /device:TPU:1, one launch (start us, length us, event | category | flops | bytes accessed | tf_op | source)
XLA Modules:
  0.0 106.8 jit_solution(5036009787144824784)
XLA Ops:
  0.0 105.1 %synthesis.1 = bf16[12,8,1536]{2,1,0:T(8,128)(2,1)} custom-call(bf16[4,32,2,8,512]{4,3,2,1,0:T(8,128)(2,1)} %control.1, f32[32,32]{1,0:T(8,128)} %root.1, f32[1,512]{1,0:T(1,128)} %bitcast.4, bf16[8,512,768]{2,1,0:T(8,128)(2,1)} %legendre.1, s32[4,128]{1,0:T(4,128)} %bitcast.5, s32[6,128]{1,0:T(8,128)} %bitcast.3, bf16[12,16,8,1536]{3,2,1,0:T(8,128)(2,1)} %perturb.1), custom_call_target="tpu_custom_call" | custom-call | tf_op jit(solution)/shard_map/synthesis/pallas_call | solution.py:220
  105.2 1.7 %copy.9 = bf16[12,8,1536]{2,1,0:T(8,128)(2,1)} copy(bf16[12,8,1536]{2,1,0:T(8,128)(2,1)} %synthesis.1) | data formatting | bytes 589824

commit v2 on v1

--- a/solution.py
+++ b/solution.py
@@ -17,24 +17,27 @@
     return jnp.dot(a, b, preferred_element_type=F32)
 
 
-def split3(a):
+def split2(a):
     hi = a.astype(BF16)
-    rest = a - hi.astype(F32)
-    mid = rest.astype(BF16)
-    low = (rest - mid.astype(F32)).astype(BF16)
-    return hi, mid, low
+    return hi, (a - hi.astype(F32)).astype(BF16)
 
 
 def spread_rows(row):
     return jnp.transpose(jnp.broadcast_to(row, (128, 128)))
 
 
-def peer(row, mem, o):
-    z, y, c = lax.div(row, 8), lax.rem(lax.div(row, 2), 4), lax.rem(row, 2)
-    z = lax.rem(z + lax.div(o, 32), 8)
-    y = lax.rem(y + lax.rem(lax.div(o, 8), 4), 4)
-    c = lax.rem(c + lax.rem(lax.div(o, 4), 2), 2)
-    return (z * 4 + y) * 2 + c, lax.rem(mem + lax.rem(o, 4), 4)
+def everyone_else(row, mem, act):
+    mems = [mem] + [lax.rem(mem + d, 4) for d in range(1, 4)]
+    for d in range(1, 4):
+        act(row, mems[d])
+
+    def whole_row(r, _):
+        for m in mems:
+            act(r, m)
+        return 0
+
+    lax.fori_loop(row + 1, 64, whole_row, 0)
+    lax.fori_loop(0, row, whole_row, 0)
 
 
 def kernel(
@@ -48,19 +51,12 @@
     for k in range(4):
         pltpu.make_async_copy(control.at[k], ctrl.at[k], in_sem.at[k]).start()
 
-    def load_leg(s, _):
+    def greet(r, m):
+        pl.semaphore_signal(barrier, inc=1, device_id=(r, m), device_id_type=MESH)
+
+    everyone_else(row, mem, greet)
+    for s in range(8):
         pltpu.make_async_copy(legendre.at[s], leg.at[s], leg_sem.at[s]).start()
-        return 0
-
-    lax.fori_loop(0, 8, load_leg, 0)
-    pltpu.make_async_copy(perturb, pert, in_sem.at[4]).start()
-
-    def greet(o, _):
-        r, m = peer(row, mem, o)
-        pl.semaphore_signal(barrier, inc=1, device_id=(r, m), device_id_type=MESH)
-        return 0
-
-    lax.fori_loop(1, 256, greet, 0)
 
     pick = (
         lax.broadcasted_iota(jnp.int32, (256, 32), 0) % 32
@@ -76,7 +72,7 @@
     )
     mix = [
         jnp.where(same, dot(dot(pick, part).astype(BF16), widen), 0.0).astype(BF16)
-        for part in split3(root[...])
+        for part in split2(root[...])
     ]
 
     for b in range(6):
@@ -98,7 +94,7 @@
     for r in range(2):
         for k in range(4):
             x = ctrl[k, :, r].reshape(256, 512)
-            mixed = (dot(mix[0], x) + dot(mix[1], x) + dot(mix[2], x)) * scale
+            mixed = (dot(mix[0], x) + dot(mix[1], x)) * scale
             sp32[:, :, k] = mixed.reshape(8, 4, 8, 512)
 
         def narrow(s, _):
@@ -114,36 +110,40 @@
 
     lax.fori_loop(0, 8, transform, 0)
 
+    pltpu.make_async_copy(perturb, pert, in_sem.at[4]).start()
     group = lane // 32
     me = mem * 64 + row
     pl.semaphore_wait(barrier, 255)
 
     def build(c, _):
-        def one(s, _):
-            picked = lax.dot_general(onehot[c], four[s], NT_DIMS, preferred_element_type=F32)
-            for r in range(2):
-                rolled = []
-                for q in range(4):
-                    part = picked[q * 64:(q + 1) * 64, r * 128:(r + 1) * 128]
-                    rolled.append(pltpu.roll(part, q * 32, 1) if q else part)
-                for level in range(4):
-                    tile = rolled[(0 - level) % 4]
-                    for g in range(1, 4):
-                        tile = jnp.where(group == g, rolled[(g - level) % 4], tile)
-                    msg[pl.ds(level * 16 + r * 8 + s, 64, stride=64), :] = tile
-            return 0
-
-        lax.fori_loop(0, 8, one, 0)
+        def some(i, _):
+            for s in (i * 4, i * 4 + 1, i * 4 + 2, i * 4 + 3):
+                picked = lax.dot_general(onehot[c], four[s], NT_DIMS, preferred_element_type=F32)
+                for r in range(2):
+                    rolled = []
+                    for q in range(4):
+                        part = picked[q * 64:(q + 1) * 64, r * 128:(r + 1) * 128]
+                        rolled.append(pltpu.roll(part, q * 32, 1) if q else part)
+                    for level in range(4):
+                        tile = rolled[(0 - level) % 4]
+                        for g in range(1, 4):
+                            tile = jnp.where(group == g, rolled[(g - level) % 4], tile)
+                        msg[pl.ds(level * 16 + r * 8 + s, 64, stride=72), :] = tile
+            return 0
+
+        lax.fori_loop(0, 2, some, 0)
 
         def pack(b, _):
-            start = pl.multiple_of(b * 512, 512)
-            snd[c, pl.ds(b * 32, 32)] = msg[pl.ds(start, 512), :].reshape(32, 16, 128).astype(BF16)
+            for j in range(8):
+                start = pl.multiple_of((b * 8 + j) * 72, 8)
+                snd[c, pl.ds(b * 32 + j * 4, 4)] = (
+                    msg[pl.ds(start, 64), :].reshape(4, 16, 128).astype(BF16)
+                )
             return 0
 
         lax.fori_loop(0, 8, pack, 0)
 
-        def send(o, _):
-            r, m = peer(row, mem, o)
+        def send(r, m):
             pltpu.make_async_remote_copy(
                 src_ref=snd.at[c, r * 4 + m],
                 dst_ref=rcv.at[c, me],
@@ -152,9 +152,8 @@
                 device_id=(r, m),
                 device_id_type=MESH,
             ).start()
-            return 0
-
-        lax.fori_loop(1, 256, send, 0)
+
+        everyone_else(row, mem, send)
         rcv[c, me] = snd[c, row * 4 + mem]
         return 0
 
@@ -232,7 +231,7 @@
             pltpu.VMEM((8, 256, 768), BF16),
             pltpu.VMEM((768, 128), F32),
             pltpu.VMEM((3, 256, 768), BF16),
-            pltpu.VMEM((4096, 128), F32),
+            pltpu.VMEM((64 * 72, 128), F32),
             pltpu.VMEM((3, 256, 16, 128), BF16),
             pltpu.VMEM((3, 256, 16, 128), BF16),
             pltpu.VMEM((512, 128), F32),

time: 107 us -> 93.7 us (0.88)
  Pallas kernels: 105 us -> 91.8 us
    pallas_call x1, Pallas kernels: 105 us -> 91.8 us  [shards(): pl.pallas_call(kernel, name='synthesis', out_shape=jax.ShapeDtypeStruct((...]
where the time goes in v2:
time: 93.7 us; the launch traced here: 93.5 us
  Pallas kernels  91.8 us (98%)
  local copies, waits for them, and re-layouts  1.69 us (2%)
    pallas_call x1, Pallas kernels, shards(): pl.pallas_call(kernel, name='synthesis', out_shape=jax.ShapeDtypeStruct((...  91.8 us

profile of v2, /device:TPU:1, one launch (start us, length us, event | category | flops | bytes accessed | tf_op | source)
XLA Modules:
  0.0 93.5 jit_solution(7745310187760259463)
XLA Ops:
  0.0 91.8 %synthesis.1 = bf16[12,8,1536]{2,1,0:T(8,128)(2,1)} custom-call(bf16[4,32,2,8,512]{4,3,2,1,0:T(8,128)(2,1)} %control.1, f32[32,32]{1,0:T(8,128)} %root.1, f32[1,512]{1,0:T(1,128)} %bitcast.4, bf16[8,512,768]{2,1,0:T(8,128)(2,1)} %legendre.1, s32[4,128]{1,0:T(4,128)} %bitcast.5, s32[6,128]{1,0:T(8,128)} %bitcast.3, bf16[12,16,8,1536]{3,2,1,0:T(8,128)(2,1)} %perturb.1), custom_call_target="tpu_custom_call" | custom-call | tf_op jit(solution)/shard_map/synthesis/pallas_call | solution.py:219
  91.9 1.7 %copy.9 = bf16[12,8,1536]{2,1,0:T(8,128)(2,1)} copy(bf16[12,8,1536]{2,1,0:T(8,128)(2,1)} %synthesis.1) | data formatting | bytes 589824

commit v3 on v2

--- a/solution.py
+++ b/solution.py
@@ -40,16 +40,49 @@
     lax.fori_loop(0, row, whole_row, 0)
 
 
+def far_first(row, mem, act):
+    z, y, c = lax.div(row, 8), lax.rem(lax.div(row, 2), 4), lax.rem(row, 2)
+    planes = [lax.rem(z + dz, 8) * 8 for dz in (4, 3, 5, 2, 6, 1, 7, 0)]
+    cores = [1 - c, c]
+    for dx in (2, 1, 3, 0):
+        m = lax.rem(mem + dx, 4)
+
+        def at(dy, skip, m=m):
+            line = lax.rem(y + dy, 4) * 2
+            for i, core in enumerate(cores):
+                for j, plane in enumerate(planes):
+                    if not (skip and i == 1 and j == 7):
+                        act(plane + line + core, m)
+
+        def step(t, _, at=at):
+            at(3 - t, False)
+            return 0
+
+        lax.fori_loop(0, 4 if dx else 3, step, 0)
+        if not dx:
+            at(0, True)
+
+
 def kernel(
-    control, root, loc, legendre, waves, order, perturb, out,
-    ctrl, leg, pert, sp32, spec, four, latf, onehot, msg, snd, rcv, wavef, basis, lhs,
-    in_sem, leg_sem, send_sem, recv_sem,
+    control, root_in, loc_in, legendre, waves_in, order_in, perturb, out_hbm,
+    root, loc, waves, order, out,
+    ctrl, leg, pert, sp32, spec, four, latf, onehot, msg, snd, rcv, wavef, basis, lhs, total,
+    in_sem, leg_sem, small_sem, out_sem, send_sem, recv_sem,
 ):
     row, mem = lax.axis_index("rows"), lax.axis_index("mem")
     barrier = pltpu.get_barrier_semaphore()
 
+    small = [
+        pltpu.make_async_copy(src, dst, small_sem.at[i])
+        for i, (src, dst) in enumerate(
+            ((root_in, root), (order_in, order), (loc_in, loc), (waves_in, waves))
+        )
+    ]
+    small[0].start()
     for k in range(4):
         pltpu.make_async_copy(control.at[k], ctrl.at[k], in_sem.at[k]).start()
+    for copy in small[1:]:
+        copy.start()
 
     def greet(r, m):
         pl.semaphore_signal(barrier, inc=1, device_id=(r, m), device_id_type=MESH)
@@ -70,11 +103,13 @@
         lax.broadcasted_iota(jnp.int32, (256, 256), 0) // 32
         == lax.broadcasted_iota(jnp.int32, (256, 256), 1) % 8
     )
+    small[0].wait()
     mix = [
         jnp.where(same, dot(dot(pick, part).astype(BF16), widen), 0.0).astype(BF16)
         for part in split2(root[...])
     ]
 
+    small[1].wait()
     for b in range(6):
         latf[b * 128:(b + 1) * 128, :] = spread_rows(order[b:b + 1, :].astype(F32))
     lane = lax.broadcasted_iota(jnp.int32, (64, 128), 1)
@@ -90,6 +125,7 @@
 
     for k in range(4):
         pltpu.make_async_copy(control.at[k], ctrl.at[k], in_sem.at[k]).wait()
+    small[2].wait()
     scale = loc[...]
     for r in range(2):
         for k in range(4):
@@ -148,17 +184,18 @@
                 src_ref=snd.at[c, r * 4 + m],
                 dst_ref=rcv.at[c, me],
                 send_sem=send_sem.at[c],
-                recv_sem=recv_sem.at[c],
+                recv_sem=recv_sem.at[c, mem],
                 device_id=(r, m),
                 device_id_type=MESH,
             ).start()
 
-        everyone_else(row, mem, send)
+        far_first(row, mem, send)
         rcv[c, me] = snd[c, row * 4 + mem]
         return 0
 
     lax.fori_loop(0, 3, build, 0)
 
+    small[3].wait()
     for b in range(4):
         wavef[b * 128:(b + 1) * 128, :] = spread_rows(waves[b:b + 1, :].astype(F32))
 
@@ -186,43 +223,56 @@
     pltpu.make_async_copy(perturb, pert, in_sem.at[4]).wait()
 
     def finish(c, _):
-        pltpu.make_async_copy(
-            rcv.at[c, pl.ds(0, 255)], rcv.at[c, pl.ds(0, 255)], recv_sem.at[c]
-        ).wait()
-        for kg in range(4):
-            lhs[kg * 128:(kg + 1) * 128, :] = jnp.transpose(
-                rcv[c, kg * 64:(kg + 1) * 64].reshape(1024, 128)
-            )
-
-        def columns(n, _):
-            cols = pl.ds(pl.multiple_of(n * 256, 256), 256)
-            field = dot(lhs[...], basis[:, cols]).astype(BF16).astype(F32)
-            field = field.reshape(4, 4, 4, 8, 256)
-            for g in range(4):
-                j = c * 4 + lax.rem(g + 4 - mem, 4)
-                weights = pert[j, :, :, cols].astype(F32).reshape(4, 4, 8, 256)
-                out[j, :, cols] = jnp.sum(field[:, g] * weights, axis=(0, 1)).astype(BF16)
-            return 0
-
-        lax.fori_loop(0, 6, columns, 0)
+        for step, dx in enumerate((2, 1, 3, 0)):
+            kg = lax.rem(mem + 4 - dx, 4)
+            landed = rcv.at[c, pl.ds(0, 64 if dx else 63)]
+            pltpu.make_async_copy(landed, landed, recv_sem.at[c, kg]).wait()
+            lhs[...] = jnp.transpose(rcv[c, pl.ds(kg * 64, 64)].reshape(1024, 128))
+
+            def columns(n, _, step=step, kg=kg):
+                cols = pl.ds(pl.multiple_of(n * 256, 256), 256)
+                field = dot(lhs[...], basis[:, cols]).astype(BF16).astype(F32)
+                field = field.reshape(4, 4, 8, 256)
+                for g in range(4):
+                    j = c * 4 + lax.rem(g + 4 - mem, 4)
+                    weights = pert[j, pl.ds(kg * 4, 4), :, cols].astype(F32)
+                    part = jnp.sum(field[g] * weights, axis=0)
+                    if step:
+                        part = part + total[g, :, cols]
+                    if step == 3:
+                        out[j, :, cols] = part.astype(BF16)
+                    else:
+                        total[g, :, cols] = part
+                return 0
+
+            lax.fori_loop(0, 6, columns, 0)
+        rows = pl.ds(c * 4, 4)
+        pltpu.make_async_copy(out.at[rows], out_hbm.at[rows], out_sem.at[c]).start()
         pltpu.make_async_copy(
             snd.at[c, pl.ds(0, 255)], snd.at[c, pl.ds(0, 255)], send_sem.at[c]
         ).wait()
         return 0
 
     lax.fori_loop(0, 3, finish, 0)
+    for c in range(3):
+        rows = pl.ds(c * 4, 4)
+        pltpu.make_async_copy(out.at[rows], out_hbm.at[rows], out_sem.at[c]).wait()
 
 
 def shards(control, vert_root, loc_spec, legendre, wave_table, lat_order, perturb):
-    vmem = pl.BlockSpec(memory_space=pltpu.VMEM)
     hbm = pl.BlockSpec(memory_space=pl.ANY)
     return pl.pallas_call(
         kernel,
         name="synthesis",
         out_shape=jax.ShapeDtypeStruct((12, 8, 1536), BF16),
-        in_specs=[hbm, vmem, vmem, hbm, vmem, vmem, hbm],
-        out_specs=vmem,
+        in_specs=[hbm] * 7,
+        out_specs=hbm,
         scratch_shapes=[
+            pltpu.VMEM((32, 32), F32),
+            pltpu.VMEM((1, 512), F32),
+            pltpu.VMEM((4, 128), jnp.int32),
+            pltpu.VMEM((6, 128), jnp.int32),
+            pltpu.VMEM((12, 8, 1536), BF16),
             pltpu.VMEM((4, 32, 2, 8, 512), BF16),
             pltpu.VMEM((8, 512, 768), BF16),
             pltpu.VMEM((12, 16, 8, 1536), BF16),
@@ -236,11 +286,14 @@
             pltpu.VMEM((3, 256, 16, 128), BF16),
             pltpu.VMEM((512, 128), F32),
             pltpu.VMEM((1024, 1536), BF16),
-            pltpu.VMEM((512, 1024), BF16),
+            pltpu.VMEM((128, 1024), BF16),
+            pltpu.VMEM((4, 8, 1536), F32),
             pltpu.SemaphoreType.DMA((5,)),
             pltpu.SemaphoreType.DMA((8,)),
+            pltpu.SemaphoreType.DMA((4,)),
             pltpu.SemaphoreType.DMA((3,)),
             pltpu.SemaphoreType.DMA((3,)),
+            pltpu.SemaphoreType.DMA((3, 4)),
         ],
         compiler_params=pltpu.CompilerParams(
             collective_id=0, has_side_effects=True, vmem_limit_bytes=60 * 1024 * 1024

time: 93.7 us -> 90.6 us (0.967)
  Pallas kernels: 91.8 us -> 88.8 us
    pallas_call x1, Pallas kernels: 91.8 us -> 88.8 us  [shards(): pl.pallas_call(kernel, name='synthesis', out_shape=jax.ShapeDtypeStruct((...]
where the time goes in v3:
time: 90.6 us; the launch traced here: 90.5 us
  Pallas kernels  88.8 us (98%)
  local copies, waits for them, and re-layouts  1.69 us (2%)
    pallas_call x1, Pallas kernels, shards(): pl.pallas_call(kernel, name='synthesis', out_shape=jax.ShapeDtypeStruct((...  88.8 us

profile of v3, /device:TPU:1, one launch (start us, length us, event | category | flops | bytes accessed | tf_op | source)
XLA Modules:
  0.0 90.5 jit_solution(15515677857028402498)
XLA Ops:
  0.0 88.8 %synthesis.1 = bf16[12,8,1536]{2,1,0:T(8,128)(2,1)} custom-call(bf16[4,32,2,8,512]{4,3,2,1,0:T(8,128)(2,1)} %control.1, f32[32,32]{1,0:T(8,128)} %root_in.1, f32[1,512]{1,0:T(1,128)} %bitcast.4, bf16[8,512,768]{2,1,0:T(8,128)(2,1)} %legendre.1, s32[4,128]{1,0:T(4,128)} %bitcast.5, s32[6,128]{1,0:T(8,128)} %bitcast.3, bf16[12,16,8,1536]{3,2,1,0:T(8,128)(2,1)} %perturb.1), custom_call_target="tpu_custom_call" | custom-call | tf_op jit(solution)/shard_map/synthesis/pallas_call | solution.py:264
  88.8 1.7 %copy.9 = bf16[12,8,1536]{2,1,0:T(8,128)(2,1)} copy(bf16[12,8,1536]{2,1,0:T(8,128)(2,1)} %synthesis.1) | data formatting | bytes 589824

commit v4 on v3

--- a/solution.py
+++ b/solution.py
@@ -114,15 +114,17 @@
         latf[b * 128:(b + 1) * 128, :] = spread_rows(order[b:b + 1, :].astype(F32))
     lane = lax.broadcasted_iota(jnp.int32, (64, 128), 1)
     lane_f = lane.astype(F32)
-    for c in range(3):
+
+    def choose(c):
         for q in range(4):
             rows = latf[pl.ds(c * 4 + q, 64, stride=12), :]
             for b in range(6):
                 hit = rows == lane_f + float(b * 128)
-                onehot[c, q * 64:(q + 1) * 64, b * 128:(b + 1) * 128] = jnp.where(
+                onehot[q * 64:(q + 1) * 64, b * 128:(b + 1) * 128] = jnp.where(
                     hit, 1.0, 0.0
                 ).astype(BF16)
 
+    choose(0)
     for k in range(4):
         pltpu.make_async_copy(control.at[k], ctrl.at[k], in_sem.at[k]).wait()
     small[2].wait()
@@ -139,12 +141,16 @@
 
         lax.fori_loop(0, 8, narrow, 0)
 
-    def transform(s, _):
+    for s in range(8):
         pltpu.make_async_copy(legendre.at[s], leg.at[s], leg_sem.at[s]).wait()
-        four[s] = dot(spec[s], leg[s]).astype(BF16)
-        return 0
-
-    lax.fori_loop(0, 8, transform, 0)
+
+    def transform(i, _):
+        for d in range(4):
+            s = i * 4 + d
+            four[s] = dot(spec[s], leg[s]).astype(BF16)
+        return 0
+
+    lax.fori_loop(0, 2, transform, 0)
 
     pltpu.make_async_copy(perturb, pert, in_sem.at[4]).start()
     group = lane // 32
@@ -152,22 +158,18 @@
     pl.semaphore_wait(barrier, 255)
 
     def build(c, _):
-        def some(i, _):
-            for s in (i * 4, i * 4 + 1, i * 4 + 2, i * 4 + 3):
-                picked = lax.dot_general(onehot[c], four[s], NT_DIMS, preferred_element_type=F32)
-                for r in range(2):
-                    rolled = []
-                    for q in range(4):
-                        part = picked[q * 64:(q + 1) * 64, r * 128:(r + 1) * 128]
-                        rolled.append(pltpu.roll(part, q * 32, 1) if q else part)
-                    for level in range(4):
-                        tile = rolled[(0 - level) % 4]
-                        for g in range(1, 4):
-                            tile = jnp.where(group == g, rolled[(g - level) % 4], tile)
-                        msg[pl.ds(level * 16 + r * 8 + s, 64, stride=72), :] = tile
-            return 0
-
-        lax.fori_loop(0, 2, some, 0)
+        for s in range(8):
+            picked = lax.dot_general(onehot[...], four[s], NT_DIMS, preferred_element_type=F32)
+            for r in range(2):
+                rolled = []
+                for q in range(4):
+                    part = picked[q * 64:(q + 1) * 64, r * 128:(r + 1) * 128]
+                    rolled.append(pltpu.roll(part, q * 32, 1) if q else part)
+                for level in range(4):
+                    tile = rolled[(0 - level) % 4]
+                    for g in range(1, 4):
+                        tile = jnp.where(group == g, rolled[(g - level) % 4], tile)
+                    msg[pl.ds(level * 16 + r * 8 + s, 64, stride=72), :] = tile
 
         def pack(b, _):
             for j in range(8):
@@ -191,6 +193,7 @@
 
         far_first(row, mem, send)
         rcv[c, me] = snd[c, row * 4 + mem]
+        choose(lax.rem(c + 1, 3))
         return 0
 
     lax.fori_loop(0, 3, build, 0)
@@ -229,8 +232,8 @@
             pltpu.make_async_copy(landed, landed, recv_sem.at[c, kg]).wait()
             lhs[...] = jnp.transpose(rcv[c, pl.ds(kg * 64, 64)].reshape(1024, 128))
 
-            def columns(n, _, step=step, kg=kg):
-                cols = pl.ds(pl.multiple_of(n * 256, 256), 256)
+            for n in range(6):
+                cols = slice(n * 256, (n + 1) * 256)
                 field = dot(lhs[...], basis[:, cols]).astype(BF16).astype(F32)
                 field = field.reshape(4, 4, 8, 256)
                 for g in range(4):
@@ -243,9 +246,6 @@
                         out[j, :, cols] = part.astype(BF16)
                     else:
                         total[g, :, cols] = part
-                return 0
-
-            lax.fori_loop(0, 6, columns, 0)
         rows = pl.ds(c * 4, 4)
         pltpu.make_async_copy(out.at[rows], out_hbm.at[rows], out_sem.at[c]).start()
         pltpu.make_async_copy(
@@ -280,7 +280,7 @@
             pltpu.VMEM((8, 256, 512), BF16),
             pltpu.VMEM((8, 256, 768), BF16),
             pltpu.VMEM((768, 128), F32),
-            pltpu.VMEM((3, 256, 768), BF16),
+            pltpu.VMEM((256, 768), BF16),
             pltpu.VMEM((64 * 72, 128), F32),
             pltpu.VMEM((3, 256, 16, 128), BF16),
             pltpu.VMEM((3, 256, 16, 128), BF16),

time: 90.6 us -> 88.9 us (0.981)
  Pallas kernels: 88.8 us -> 87.1 us
    pallas_call x1, Pallas kernels: 88.8 us -> 87.1 us  [shards(): pl.pallas_call(kernel, name='synthesis', out_shape=jax.ShapeDtypeStruct((...]
where the time goes in v4:
time: 88.9 us; the launch traced here: 88.8 us
  Pallas kernels  87.1 us (98%)
  local copies, waits for them, and re-layouts  1.69 us (2%)
    pallas_call x1, Pallas kernels, shards(): pl.pallas_call(kernel, name='synthesis', out_shape=jax.ShapeDtypeStruct((...  87.1 us

profile of v4, /device:TPU:1, one launch (start us, length us, event | category | flops | bytes accessed | tf_op | source)
XLA Modules:
  0.0 88.8 jit_solution(1199308712140065240)
XLA Ops:
  0.0 87.1 %synthesis.1 = bf16[12,8,1536]{2,1,0:T(8,128)(2,1)} custom-call(bf16[4,32,2,8,512]{4,3,2,1,0:T(8,128)(2,1)} %control.1, f32[32,32]{1,0:T(8,128)} %root_in.1, f32[1,512]{1,0:T(1,128)} %bitcast.4, bf16[8,512,768]{2,1,0:T(8,128)(2,1)} %legendre.1, s32[4,128]{1,0:T(4,128)} %bitcast.5, s32[6,128]{1,0:T(8,128)} %bitcast.3, bf16[12,16,8,1536]{3,2,1,0:T(8,128)(2,1)} %perturb.1), custom_call_target="tpu_custom_call" | custom-call | tf_op jit(solution)/shard_map/synthesis/pallas_call | solution.py:264
  87.1 1.7 %copy.9 = bf16[12,8,1536]{2,1,0:T(8,128)(2,1)} copy(bf16[12,8,1536]{2,1,0:T(8,128)(2,1)} %synthesis.1) | data formatting | bytes 589824

commit v5 on v4

--- a/solution.py
+++ b/solution.py
@@ -66,7 +66,7 @@
 def kernel(
     control, root_in, loc_in, legendre, waves_in, order_in, perturb, out_hbm,
     root, loc, waves, order, out,
-    ctrl, leg, pert, sp32, spec, four, latf, onehot, msg, snd, rcv, wavef, basis, lhs, total,
+    ctrl, leg, pert, sp32, spec, four, latf, mixing, onehot, msg, snd, rcv, wavef, basis, lhs, total,
     in_sem, leg_sem, small_sem, out_sem, send_sem, recv_sem,
 ):
     row, mem = lax.axis_index("rows"), lax.axis_index("mem")
@@ -84,12 +84,16 @@
     for copy in small[1:]:
         copy.start()
 
+    def load_leg(half):
+        for s in range(half * 4, half * 4 + 4):
+            pltpu.make_async_copy(legendre.at[s], leg.at[s], leg_sem.at[s]).start()
+
     def greet(r, m):
         pl.semaphore_signal(barrier, inc=1, device_id=(r, m), device_id_type=MESH)
 
+    load_leg(0)
     everyone_else(row, mem, greet)
-    for s in range(8):
-        pltpu.make_async_copy(legendre.at[s], leg.at[s], leg_sem.at[s]).start()
+    load_leg(1)
 
     pick = (
         lax.broadcasted_iota(jnp.int32, (256, 32), 0) % 32
@@ -108,6 +112,9 @@
         jnp.where(same, dot(dot(pick, part).astype(BF16), widen), 0.0).astype(BF16)
         for part in split2(root[...])
     ]
+    for half in range(2):
+        for i, part in enumerate(mix):
+            mixing[half, i * 128:(i + 1) * 128, :] = part[half * 128:(half + 1) * 128, :]
 
     small[1].wait()
     for b in range(6):
@@ -125,41 +132,31 @@
                 ).astype(BF16)
 
     choose(0)
-    for k in range(4):
-        pltpu.make_async_copy(control.at[k], ctrl.at[k], in_sem.at[k]).wait()
-    small[2].wait()
-    scale = loc[...]
-    for r in range(2):
-        for k in range(4):
-            x = ctrl[k, :, r].reshape(256, 512)
-            mixed = (dot(mix[0], x) + dot(mix[1], x)) * scale
-            sp32[:, :, k] = mixed.reshape(8, 4, 8, 512)
-
-        def narrow(s, _):
-            spec[s, r * 128:(r + 1) * 128, :] = sp32[s].reshape(128, 512).astype(BF16)
-            return 0
-
-        lax.fori_loop(0, 8, narrow, 0)
-
-    for s in range(8):
-        pltpu.make_async_copy(legendre.at[s], leg.at[s], leg_sem.at[s]).wait()
-
-    def transform(i, _):
-        for d in range(4):
-            s = i * 4 + d
-            four[s] = dot(spec[s], leg[s]).astype(BF16)
-        return 0
-
-    lax.fori_loop(0, 2, transform, 0)
-
-    pltpu.make_async_copy(perturb, pert, in_sem.at[4]).start()
     group = lane // 32
     me = mem * 64 + row
-    pl.semaphore_wait(barrier, 255)
-
-    def build(c, _):
-        for s in range(8):
-            picked = lax.dot_general(onehot[...], four[s], NT_DIMS, preferred_element_type=F32)
+
+    def transform(half):
+        for r in range(2):
+            for k in range(4):
+                if not half and not r:
+                    pltpu.make_async_copy(control.at[k], ctrl.at[k], in_sem.at[k]).wait()
+                both = dot(mixing[half], ctrl[k, :, r].reshape(256, 512))
+                mixed = (both[:128] + both[128:]) * scale
+                sp32[:, :, k] = mixed.reshape(4, 4, 8, 512)
+
+            for s in range(4):
+                spec[s, r * 128:(r + 1) * 128, :] = sp32[s].reshape(128, 512).astype(BF16)
+
+        for s in range(half * 4, half * 4 + 4):
+            pltpu.make_async_copy(legendre.at[s], leg.at[s], leg_sem.at[s]).wait()
+        for s in range(4):
+            four[half * 4 + s] = dot(spec[s], leg[half * 4 + s]).astype(BF16)
+
+    def gather(half):
+        for s in range(4):
+            picked = lax.dot_general(
+                onehot[...], four[half * 4 + s], NT_DIMS, preferred_element_type=F32
+            )
             for r in range(2):
                 rolled = []
                 for q in range(4):
@@ -169,60 +166,94 @@
                     tile = rolled[(0 - level) % 4]
                     for g in range(1, 4):
                         tile = jnp.where(group == g, rolled[(g - level) % 4], tile)
-                    msg[pl.ds(level * 16 + r * 8 + s, 64, stride=72), :] = tile
+                    start = level * 16 + half * 8 + r * 4 + s
+                    msg[pl.ds(start, 64, stride=72), :] = tile
+
+    def send(src, dst, c, r, m):
+        pltpu.make_async_remote_copy(
+            src_ref=src,
+            dst_ref=dst,
+            send_sem=send_sem.at[c],
+            recv_sem=recv_sem.at[c, mem],
+            device_id=(r, m),
+            device_id_type=MESH,
+        ).start()
+
+    small[2].wait()
+    scale = loc[...]
+    for half in range(2):
+        transform(half)
+        gather(half)
+
+        def pack_half(b, _, half=half):
+            for j in range(8):
+                for level in range(4):
+                    start = pl.multiple_of((b * 8 + j) * 72 + level * 16 + half * 8, 8)
+                    snd[0, b * 32 + j * 4 + level, half] = msg[pl.ds(start, 8), :].astype(BF16)
+            return 0
+
+        lax.fori_loop(0, 8, pack_half, 0)
+        if not half:
+            pl.semaphore_wait(barrier, 255)
+
+        def send_half(r, m, half=half):
+            send(snd.at[0, r * 4 + m, half], rcv.at[0, me, half], 0, r, m)
+
+        far_first(row, mem, send_half)
+    pltpu.make_async_copy(perturb, pert, in_sem.at[4]).start()
+    rcv[0, me] = snd[0, row * 4 + mem]
+
+    def build(c, _):
+        choose(c)
+        for half in range(2):
+            gather(half)
 
         def pack(b, _):
             for j in range(8):
                 start = pl.multiple_of((b * 8 + j) * 72, 8)
                 snd[c, pl.ds(b * 32 + j * 4, 4)] = (
-                    msg[pl.ds(start, 64), :].reshape(4, 16, 128).astype(BF16)
+                    msg[pl.ds(start, 64), :].reshape(4, 2, 8, 128).astype(BF16)
                 )
             return 0
 
         lax.fori_loop(0, 8, pack, 0)
 
-        def send(r, m):
-            pltpu.make_async_remote_copy(
-                src_ref=snd.at[c, r * 4 + m],
-                dst_ref=rcv.at[c, me],
-                send_sem=send_sem.at[c],
-                recv_sem=recv_sem.at[c, mem],
-                device_id=(r, m),
-                device_id_type=MESH,
-            ).start()
-
-        far_first(row, mem, send)
+        def send_tile(r, m):
+            send(snd.at[c, r * 4 + m], rcv.at[c, me], c, r, m)
+
+        far_first(row, mem, send_tile)
         rcv[c, me] = snd[c, row * 4 + mem]
-        choose(lax.rem(c + 1, 3))
         return 0
 
-    lax.fori_loop(0, 3, build, 0)
+    lax.fori_loop(1, 3, build, 0)
 
     small[3].wait()
     for b in range(4):
-        wavef[b * 128:(b + 1) * 128, :] = spread_rows(waves[b:b + 1, :].astype(F32))
-
-    def angles(wave, step):
-        phase = wave * step
+        latf[b * 128:(b + 1) * 128, :] = spread_rows(waves[b:b + 1, :].astype(F32))
+    for s in range(4):
+        wave = latf[pl.ds(s, 128, stride=4), :]
+        for r in range(2):
+            wavef[pl.ds(r * 4 + s, 128, stride=8), :] = wave
+    turn = ((lax.broadcasted_iota(jnp.int32, (64, 128), 0) // 4) % 2).astype(F32) * 384.0
+
+    def angles(phase):
         phase = phase - 1536.0 * jnp.floor(phase * (1.0 / 1536.0))
         return phase * (2.0 * math.pi / 1536.0)
 
     def make_basis(b, _):
-        wave = wavef[pl.ds(pl.multiple_of(b * 64, 64), 64), :]
+        rows = pl.ds(pl.multiple_of(b * 64, 64), 64)
+        wave = wavef[rows, :]
         weight = jnp.where(wave == 0.0, 1.0, 2.0)
-        near = angles(wave, lane_f)
-        far = angles(wave, 128.0)
+        near = angles(wave * lane_f + turn)
+        far = angles(wave * 128.0)
         cos, sin = weight * jnp.cos(near), weight * jnp.sin(near)
         turn_cos, turn_sin = jnp.cos(far), jnp.sin(far)
         for a in range(12):
-            pair = jnp.stack([cos.reshape(8, 8, 128), -sin.reshape(8, 8, 128)], axis=1)
-            basis[pl.ds(pl.multiple_of(b * 128, 128), 128), a * 128:(a + 1) * 128] = (
-                pair.reshape(128, 128).astype(BF16)
-            )
+            basis[rows, a * 128:(a + 1) * 128] = cos.astype(BF16)
             cos, sin = cos * turn_cos - sin * turn_sin, sin * turn_cos + cos * turn_sin
         return 0
 
-    lax.fori_loop(0, 8, make_basis, 0)
+    lax.fori_loop(0, 16, make_basis, 0)
     pltpu.make_async_copy(perturb, pert, in_sem.at[4]).wait()
 
     def finish(c, _):
@@ -276,15 +307,16 @@
             pltpu.VMEM((4, 32, 2, 8, 512), BF16),
             pltpu.VMEM((8, 512, 768), BF16),
             pltpu.VMEM((12, 16, 8, 1536), BF16),
-            pltpu.VMEM((8, 4, 4, 8, 512), F32),
-            pltpu.VMEM((8, 256, 512), BF16),
+            pltpu.VMEM((4, 4, 4, 8, 512), F32),
+            pltpu.VMEM((4, 256, 512), BF16),
             pltpu.VMEM((8, 256, 768), BF16),
             pltpu.VMEM((768, 128), F32),
+            pltpu.VMEM((2, 256, 256), BF16),
             pltpu.VMEM((256, 768), BF16),
             pltpu.VMEM((64 * 72, 128), F32),
-            pltpu.VMEM((3, 256, 16, 128), BF16),
-            pltpu.VMEM((3, 256, 16, 128), BF16),
-            pltpu.VMEM((512, 128), F32),
+            pltpu.VMEM((3, 256, 2, 8, 128), BF16),
+            pltpu.VMEM((3, 256, 2, 8, 128), BF16),
+            pltpu.VMEM((1024, 128), F32),
             pltpu.VMEM((1024, 1536), BF16),
             pltpu.VMEM((128, 1024), BF16),
             pltpu.VMEM((4, 8, 1536), F32),

time: 88.9 us -> 87.2 us (0.981)
  Pallas kernels: 87.1 us -> 85.4 us
    pallas_call x1, Pallas kernels: 87.1 us -> 85.4 us  [shards(): pl.pallas_call(kernel, name='synthesis', out_shape=jax.ShapeDtypeStruct((...]
where the time goes in v5:
time: 87.2 us; the launch traced here: 87.1 us
  Pallas kernels  85.4 us (98%)
  local copies, waits for them, and re-layouts  1.69 us (2%)
    pallas_call x1, Pallas kernels, shards(): pl.pallas_call(kernel, name='synthesis', out_shape=jax.ShapeDtypeStruct((...  85.4 us

profile of v5, /device:TPU:1, one launch (start us, length us, event | category | flops | bytes accessed | tf_op | source)
XLA Modules:
  0.0 87.1 jit_solution(15865404129681585431)
XLA Ops:
  0.0 85.4 %synthesis.1 = bf16[12,8,1536]{2,1,0:T(8,128)(2,1)} custom-call(bf16[4,32,2,8,512]{4,3,2,1,0:T(8,128)(2,1)} %control.1, f32[32,32]{1,0:T(8,128)} %root_in.1, f32[1,512]{1,0:T(1,128)} %bitcast.4, bf16[8,512,768]{2,1,0:T(8,128)(2,1)} %legendre.1, s32[4,128]{1,0:T(4,128)} %bitcast.5, s32[6,128]{1,0:T(8,128)} %bitcast.3, bf16[12,16,8,1536]{3,2,1,0:T(8,128)(2,1)} %perturb.1), custom_call_target="tpu_custom_call" | custom-call | tf_op jit(solution)/shard_map/synthesis/pallas_call | solution.py:295
  85.4 1.7 %copy.9 = bf16[12,8,1536]{2,1,0:T(8,128)(2,1)} copy(bf16[12,8,1536]{2,1,0:T(8,128)(2,1)} %synthesis.1) | data formatting | bytes 589824

commit v6 on v5

--- a/solution.py
+++ b/solution.py
@@ -64,10 +64,10 @@
 
 
 def kernel(
-    control, root_in, loc_in, legendre, waves_in, order_in, perturb, out_hbm,
-    root, loc, waves, order, out,
+    control, root_in, loc_in, legendre, waves_in, order_in, perturb, out,
+    root, loc, waves, order,
     ctrl, leg, pert, sp32, spec, four, latf, mixing, onehot, msg, snd, rcv, wavef, basis, lhs, total,
-    in_sem, leg_sem, small_sem, out_sem, send_sem, recv_sem,
+    in_sem, leg_sem, small_sem, send_sem, recv_sem,
 ):
     row, mem = lax.axis_index("rows"), lax.axis_index("mem")
     barrier = pltpu.get_barrier_semaphore()
@@ -277,17 +277,12 @@
                         out[j, :, cols] = part.astype(BF16)
                     else:
                         total[g, :, cols] = part
-        rows = pl.ds(c * 4, 4)
-        pltpu.make_async_copy(out.at[rows], out_hbm.at[rows], out_sem.at[c]).start()
         pltpu.make_async_copy(
             snd.at[c, pl.ds(0, 255)], snd.at[c, pl.ds(0, 255)], send_sem.at[c]
         ).wait()
         return 0
 
     lax.fori_loop(0, 3, finish, 0)
-    for c in range(3):
-        rows = pl.ds(c * 4, 4)
-        pltpu.make_async_copy(out.at[rows], out_hbm.at[rows], out_sem.at[c]).wait()
 
 
 def shards(control, vert_root, loc_spec, legendre, wave_table, lat_order, perturb):
@@ -295,15 +290,14 @@
     return pl.pallas_call(
         kernel,
         name="synthesis",
-        out_shape=jax.ShapeDtypeStruct((12, 8, 1536), BF16),
+        out_shape=pltpu.VMEM((12, 8, 1536), BF16),
         in_specs=[hbm] * 7,
-        out_specs=hbm,
+        out_specs=pl.BlockSpec(memory_space=pltpu.VMEM),
         scratch_shapes=[
             pltpu.VMEM((32, 32), F32),
             pltpu.VMEM((1, 512), F32),
             pltpu.VMEM((4, 128), jnp.int32),
             pltpu.VMEM((6, 128), jnp.int32),
-            pltpu.VMEM((12, 8, 1536), BF16),
             pltpu.VMEM((4, 32, 2, 8, 512), BF16),
             pltpu.VMEM((8, 512, 768), BF16),
             pltpu.VMEM((12, 16, 8, 1536), BF16),
@@ -324,7 +318,6 @@
             pltpu.SemaphoreType.DMA((8,)),
             pltpu.SemaphoreType.DMA((4,)),
             pltpu.SemaphoreType.DMA((3,)),
-            pltpu.SemaphoreType.DMA((3,)),
             pltpu.SemaphoreType.DMA((3, 4)),
         ],
         compiler_params=pltpu.CompilerParams(

time: 87.2 us -> 85.5 us (0.981)
  local copies, waits for them, and re-layouts: 1.69 us -> 0.72 us
    unnamed x1, local copies, waits for them, and re-layouts: 1.69 us -> 0.72 us
where the time goes in v6:
time: 85.5 us
  Pallas kernels  84.7 us (99%)
    pallas_call x1, Pallas kernels, shards(): pl.pallas_call(kernel, name='synthesis', out_shape=pltpu.VMEM((12, 8, 153...  84.7 us

profile of v6, /device:TPU:1, one launch (start us, length us, event | category | flops | bytes accessed | tf_op | source)
XLA Modules:
  0.0 85.5 jit_solution(5579388430240462695)
XLA Ops:
  0.0 84.7 %synthesis.1 = bf16[12,8,1536]{2,1,0:T(8,128)(2,1)S(1)} custom-call(bf16[4,32,2,8,512]{4,3,2,1,0:T(8,128)(2,1)} %control.1, f32[32,32]{1,0:T(8,128)} %root_in.1, f32[1,512]{1,0:T(1,128)} %bitcast.4, bf16[8,512,768]{2,1,0:T(8,128)(2,1)} %legendre.1, s32[4,128]{1,0:T(4,128)} %bitcast.5, s32[6,128]{1,0:T(8,128)} %bitcast.3, bf16[12,16,8,1536]{3,2,1,0:T(8,128)(2,1)} %perturb.1), custom_call_target="tpu_custom_call" | custom-call | tf_op jit(solution)/shard_map/synthesis/pallas_call | solution.py:290
  84.8 0.7 copy.9

commit v7 on v6

--- a/solution.py
+++ b/solution.py
@@ -26,7 +26,7 @@
     return jnp.transpose(jnp.broadcast_to(row, (128, 128)))
 
 
-def everyone_else(row, mem, act):
+def everyone_else(row, mem, act, between):
     mems = [mem] + [lax.rem(mem + d, 4) for d in range(1, 4)]
     for d in range(1, 4):
         act(row, mems[d])
@@ -37,6 +37,7 @@
         return 0
 
     lax.fori_loop(row + 1, 64, whole_row, 0)
+    between()
     lax.fori_loop(0, row, whole_row, 0)
 
 
@@ -61,6 +62,27 @@
         lax.fori_loop(0, 4 if dx else 3, step, 0)
         if not dx:
             at(0, True)
+
+
+def far_first_mixed(row, mem, act):
+    z, y, c = lax.div(row, 8), lax.rem(lax.div(row, 2), 4), lax.rem(row, 2)
+    planes = [lax.rem(z + dz, 8) * 8 for dz in (4, 3, 5, 2, 6, 1, 7, 0)]
+    mems = [lax.rem(mem + dx, 4) for dx in (2, 1, 3)] + [mem]
+
+    def at(dy, core, skip):
+        line = lax.rem(y + dy, 4) * 2 + core
+        for j, plane in enumerate(planes):
+            for i, m in enumerate(mems):
+                if not (skip and j == 7 and i == 3):
+                    act(plane + line, m)
+
+    def step(t, _):
+        dy = 3 - lax.div(t, 2)
+        at(dy, lax.rem(c + 1 + t, 2), False)
+        return 0
+
+    lax.fori_loop(0, 7, step, 0)
+    at(0, c, True)
 
 
 def kernel(
@@ -91,8 +113,7 @@
     def greet(r, m):
         pl.semaphore_signal(barrier, inc=1, device_id=(r, m), device_id_type=MESH)
 
-    load_leg(0)
-    everyone_else(row, mem, greet)
+    everyone_else(row, mem, greet, lambda: load_leg(0))
     load_leg(1)
 
     pick = (
@@ -138,8 +159,6 @@
     def transform(half):
         for r in range(2):
             for k in range(4):
-                if not half and not r:
-                    pltpu.make_async_copy(control.at[k], ctrl.at[k], in_sem.at[k]).wait()
                 both = dot(mixing[half], ctrl[k, :, r].reshape(256, 512))
                 mixed = (both[:128] + both[128:]) * scale
                 sp32[:, :, k] = mixed.reshape(4, 4, 8, 512)
@@ -181,6 +200,8 @@
 
     small[2].wait()
     scale = loc[...]
+    for k in range(4):
+        pltpu.make_async_copy(control.at[k], ctrl.at[k], in_sem.at[k]).wait()
     for half in range(2):
         transform(half)
         gather(half)
@@ -199,7 +220,7 @@
         def send_half(r, m, half=half):
             send(snd.at[0, r * 4 + m, half], rcv.at[0, me, half], 0, r, m)
 
-        far_first(row, mem, send_half)
+        far_first_mixed(row, mem, send_half)
     pltpu.make_async_copy(perturb, pert, in_sem.at[4]).start()
     rcv[0, me] = snd[0, row * 4 + mem]
 

time: 85.5 us -> 85.5 us (level)
  no operation moved by 1% of the time
where the time goes in v7:
time: 85.5 us
  Pallas kernels  84.7 us (99%)
    pallas_call x1, Pallas kernels, shards(): pl.pallas_call(kernel, name='synthesis', out_shape=pltpu.VMEM((12, 8, 153...  84.7 us

profile of v7, /device:TPU:1, one launch (start us, length us, event | category | flops | bytes accessed | tf_op | source)
XLA Modules:
  0.0 85.5 jit_solution(7941843865352578395)
XLA Ops:
  0.0 84.7 %synthesis.1 = bf16[12,8,1536]{2,1,0:T(8,128)(2,1)S(1)} custom-call(bf16[4,32,2,8,512]{4,3,2,1,0:T(8,128)(2,1)} %control.1, f32[32,32]{1,0:T(8,128)} %root_in.1, f32[1,512]{1,0:T(1,128)} %bitcast.4, bf16[8,512,768]{2,1,0:T(8,128)(2,1)} %legendre.1, s32[4,128]{1,0:T(4,128)} %bitcast.5, s32[6,128]{1,0:T(8,128)} %bitcast.3, bf16[12,16,8,1536]{3,2,1,0:T(8,128)(2,1)} %perturb.1), custom_call_target="tpu_custom_call" | custom-call | tf_op jit(solution)/shard_map/synthesis/pallas_call | solution.py:311
  84.7 0.7 copy.9

commit v8 on v7

--- a/solution.py
+++ b/solution.py
@@ -224,7 +224,7 @@
     pltpu.make_async_copy(perturb, pert, in_sem.at[4]).start()
     rcv[0, me] = snd[0, row * 4 + mem]
 
-    def build(c, _):
+    def build(c):
         choose(c)
         for half in range(2):
             gather(half)
@@ -242,11 +242,11 @@
         def send_tile(r, m):
             send(snd.at[c, r * 4 + m], rcv.at[c, me], c, r, m)
 
-        far_first(row, mem, send_tile)
+        (far_first_mixed if c == 1 else far_first)(row, mem, send_tile)
         rcv[c, me] = snd[c, row * 4 + mem]
-        return 0
-
-    lax.fori_loop(1, 3, build, 0)
+
+    for c in (1, 2):
+        build(c)
 
     small[3].wait()
     for b in range(4):

time: 85.5 us -> 85.5 us (level)
  no operation moved by 1% of the time
where the time goes in v8:
time: 85.5 us
  Pallas kernels  84.7 us (99%)
    pallas_call x1, Pallas kernels, shards(): pl.pallas_call(kernel, name='synthesis', out_shape=pltpu.VMEM((12, 8, 153...  84.7 us

profile of v8, /device:TPU:1, one launch (start us, length us, event | category | flops | bytes accessed | tf_op | source)
XLA Modules:
  0.0 85.5 jit_solution(10104891185393133803)
XLA Ops:
  0.0 84.7 %synthesis.1 = bf16[12,8,1536]{2,1,0:T(8,128)(2,1)S(1)} custom-call(bf16[4,32,2,8,512]{4,3,2,1,0:T(8,128)(2,1)} %control.1, f32[32,32]{1,0:T(8,128)} %root_in.1, f32[1,512]{1,0:T(1,128)} %bitcast.4, bf16[8,512,768]{2,1,0:T(8,128)(2,1)} %legendre.1, s32[4,128]{1,0:T(4,128)} %bitcast.5, s32[6,128]{1,0:T(8,128)} %bitcast.3, bf16[12,16,8,1536]{3,2,1,0:T(8,128)(2,1)} %perturb.1), custom_call_target="tpu_custom_call" | custom-call | tf_op jit(solution)/shard_map/synthesis/pallas_call | solution.py:311
  84.7 0.7 copy.9
